TPU v7x, 32 devices: a whole 2x2x4 slice. The times are simulated.
32 devices in a mesh: row: 8 (over z, y), col: 4 (over x, core).
Axes of the slice: x: 2, y: 2, z: 4, core: 2. Of those that a mesh axis runs over, the one named last changes fastest.
Arguments:
- new_dosage: float32 [4096, 1024], P(('col', 'row')), may hold values from 0 to 2
- old_dosage: float32 [16384, 1024], P(('row', 'col')), may hold values from 0 to 2
- grm: bfloat16 [16384, 4096], P('row', 'col'), may hold values from -1.5 to 1.5
- counts: int32 [8], P('col'), may hold values from 256 to 512
- affected: int32 [32, 8], P('row', 'col'), may hold values from 0 to 1, as said below
Outputs:
- updated: bfloat16 [16384, 4096], P('row', 'col')
Inputs may be any that keep to these rules, and one draw needn't show every extreme that they name: `affected`: the density of marked tile pairs differs from one tile of new samples to the next.
All inputs are finite; a program needn't handle non-finite values.
Results may differ from a plain program's by a relative error of at most 0.00115.
Values may be sent and summed in bfloat16 or wider, within the bound.
A program may use at most 128 MiB of HBM per device.

v0:
```python
import jax
import jax.numpy as jnp
from jax import lax
from jax.sharding import PartitionSpec as P

TILE = 512


def on_device(new_dosage, old_dosage, grm, counts, affected):
    devices = lax.axis_size("row") * lax.axis_size("col")
    totals = lax.psum(jnp.sum(old_dosage, axis=0), ("row", "col"))
    doubled = totals / (old_dosage.shape[0] * devices)
    spread = jnp.sqrt(doubled * (1.0 - 0.5 * doubled) + 0.1)
    usable = (jnp.arange(TILE)[None, :] < counts[:, None]).reshape(-1).astype(jnp.float32)
    snp_count = new_dosage.shape[1]
    contract = (((1,), (1,)), ((), ()))
    local_rows = new_dosage.shape[0]
    usable_mine = lax.dynamic_slice_in_dim(usable, lax.axis_index("row") * local_rows, local_rows)
    scores_mine = ((new_dosage - doubled) / spread * usable_mine[:, None]).astype(jnp.bfloat16)
    new_scores = lax.all_gather(scores_mine, "row", axis=0, tiled=True)
    old_mine = ((old_dosage - doubled) / spread).astype(jnp.bfloat16)
    product = lax.dot_general(
        lax.all_gather(old_mine, "col", axis=0, tiled=True),
        new_scores,
        contract,
        preferred_element_type=jnp.float32,
    )
    row_count, col_count = product.shape
    scaled = (product / snp_count).reshape(row_count // TILE, TILE, col_count // TILE, TILE)
    masked_update = scaled * affected.astype(jnp.float32)[:, None, :, None]
    return (grm.astype(jnp.float32) + masked_update.reshape(row_count, col_count)).astype(
        jnp.bfloat16
    )


def solution(mesh):
    in_specs = (
        P(("col", "row"), None),
        P(("row", "col"), None),
        P("row", "col"),
        P("col"),
        P("row", "col"),
    )
    out_specs = P("row", "col")
    return jax.shard_map(
        on_device, mesh=mesh, in_specs=in_specs, out_specs=out_specs, check_vma=False
    )
```

profile of v0, /device:TPU:0, one launch (start us, length us, event | category | flops | bytes accessed | tf_op | source)
XLA Modules:
  0.0 157.1 jit_solution(6402705490686522627)
XLA Ops:
  6.5 0.0 copy-start
  6.5 0.0 copy-start.1
  6.5 0.0 all-gather.5.cloned.1.call-start
  6.5 1.9 %reduce_sum.9 = f32[1024]{0:T(1024)S(1)} reduce(f32[512,1024]{1,0:T(8,128)} %param.6, f32[]{:T(128)} %constant.5.clone.1), dimensions={0}, to_apply=%region_0.0 | reduce | flops 523264 | bytes 2101252 | tf_op jit(solution)/shard_map/reduce_sum | solution.py:11
  8.4 42.0 %psum.7 = f32[1024]{0:T(1024)S(1)} all-reduce(f32[1024]{0:T(1024)S(1)} %reduce_sum.9), channel_id=1, replica_groups=mesh['row'=8,'col'=4] {'row','col'}, use_global_device_ids=true, to_apply=%region_1.0 | all-reduce | flops 1024 | bytes 8192 | tf_op jit(solution)/shard_map/psum | solution.py:11
  50.5 0.7 fusion
  51.2 0.1 dynamic_slice.3
  51.3 1.8 %multiply_convert_fusion = bf16[128,1024]{1,0:T(8,128)(2,1)} fusion(f32[128,1024]{1,0:T(8,128)} %param.5, f32[128]{0:T(128)S(1)} %dynamic_slice.3, f32[1024]{0:T(1024)S(1)} %get-tuple-element.6, f32[1024]{0:T(1024)S(1)} %get-tuple-element.5), kind=kLoop, calls=%fused_computation.2 | loop fusion | flops 524288 | bytes 795136 | tf_op jit(solution)/shard_map/convert_element_type | solution.py:19
  53.1 0.0 all-gather.5.cloned.1.call-update
  53.1 0.0 all-gather.3.cloned.1.call-start
  53.2 0.0 copy-done
  53.2 1.3 divide_convert_fusion
  54.5 0.0 all-gather.3.cloned.1.call-update
  54.5 0.0 copy-done.1
  54.5 0.1 copy.6
  54.6 5.5 %mul.37 = f32[4,512,2,512]{3,2,1,0:T(2,128)} broadcast(f32[4,2]{1,0:T(4,128)S(1)} %copy.6), dimensions={0,2} | broadcast | bytes 8388640 | tf_op jit(solution)/shard_map/mul | solution.py:30
  60.1 8.9 %copy.8 = f32[256,8,2,512]{3,1,2,0:T(8,128)} copy(f32[256,8,2,512]{3,2,1,0:T(2,128)} %bitcast.8) | data formatting | bytes 16777216
  68.9 33.3 %all-gather.5.cloned.1.call-done = bf16[1024,1024]{1,0:T(8,128)(2,1)} async-done(((bf16[128,1024]{1,0:T(8,128)(2,1)}), bf16[1024,1024]{1,0:T(8,128)(2,1)}) %all-gather.5.cloned.1.call-update) | async-done | bytes 2097168 | tf_op jit(solution)/shard_map/all_gather | solution.py:20
  102.2 34.6 %all-gather.3.cloned.1.call-done = bf16[2048,1024]{1,0:T(8,128)(2,1)} async-done(((bf16[512,1024]{1,0:T(8,128)(2,1)}), bf16[2048,1024]{1,0:T(8,128)(2,1)}) %all-gather.3.cloned.1.call-update) | async-done | bytes 4194320 | tf_op jit(solution)/shard_map/all_gather | solution.py:23
  136.8 13.5 %add_convert_fusion = bf16[2048,1024]{1,0:T(8,128)(2,1)} fusion(f32[2048,1024]{1,0:T(8,128)} %bitcast.9, bf16[2048,1024]{1,0:T(8,128)(2,1)} %param.7, bf16[2048,1024]{1,0:T(8,128)(2,1)} %all-gather.3.cloned.1.call-done, bf16[1024,1024]{1,0:T(8,128)(2,1)} %all-gather.5.cloned.1.call-done), kind=kOutput, calls=%fused_computation | convolution fusion | flops 4305453056 | bytes 23068672 | tf_op jit(solution)/shard_map/dot_general | solution.py:22
  (3 shorter events, 0.0 us)
Async XLA Ops:
  6.5 46.7 %copy-start = (f32[512,1024]{1,0:T(8,128)S(1)}, f32[512,1024]{1,0:T(8,128)}, u32[]{:S(2)}) copy-start(f32[512,1024]{1,0:T(8,128)} %param.6) | copy-start | bytes 6291460
  6.5 48.0 %copy-start.1 = (s32[4,2]{0,1:T(2,128)S(1)}, s32[4,2]{0,1:T(2,128)}, u32[]{:S(2)}) copy-start(s32[4,2]{0,1:T(2,128)} %param.9) | copy-start | bytes 100
  6.5 95.6 %all-gather.5.cloned.1.call-start = ((), (), s32[]{:S(2)}) async-start(), calls=%async_computation.1 | async-start | bytes 2359296 | tf_op jit(solution)/shard_map/all_gather | solution.py:20
  53.1 83.6 %all-gather.3.cloned.1.call-start = ((), (), s32[]{:S(2)}) async-start(), calls=%async_computation | async-start | bytes 5242880 | tf_op jit(solution)/shard_map/all_gather | solution.py:23
Sparse Core Ops, SparseCore 0:
  53.3 48.8 all-gather.4
  103.7 32.9 all-gather.2
where the time goes:
time: 157 us
  waiting for transfers between devices  67.9 us (43%)
  blocking collectives  42 us (27%)
  local copies, waits for them, and re-layouts  14.5 us (9%)
  matrix products  13.5 us (9%)
  between operations  13.4 us (9%)
  other arithmetic  5.75 us (4%)
    psum x1, blocking collectives, on_device(): totals = lax.psum(jnp.sum(old_dosage, axis=0), ('row', 'col'))  42 us
    all_gather x1, waiting for transfers between devices, on_device(): lax.all_gather(old_mine, 'col', axis=0, tiled=True)  34.6 us
    all_gather x1, waiting for transfers between devices, on_device(): new_scores = lax.all_gather(scores_mine, 'row', axis=0, tiled=True)  33.3 us
    dot_general x1, matrix products, on_device(): lax.dot_general(lax.all_gather(old_mine, 'col', axis=0, tiled=True), new_...  13.5 us
    unnamed x6, local copies, waits for them, and re-layouts  8.87 us
    mul x1, local copies, waits for them, and re-layouts, on_device(): masked_update = scaled * affected.astype(jnp.float32)[:, None, :, None]  5.45 us
  transfers between devices with their start and end apart: 2, of which 2 were waited for; matrix products, arithmetic and copies ran while one was open for 10% of the time, Pallas kernels for 0%

commit v1 on v0

--- a/solution.py
+++ b/solution.py
@@ -8,7 +8,7 @@
 
 def on_device(new_dosage, old_dosage, grm, counts, affected):
     devices = lax.axis_size("row") * lax.axis_size("col")
-    totals = lax.psum(jnp.sum(old_dosage, axis=0), ("row", "col"))
+    totals = jnp.sum(jax.lax.all_gather(jnp.sum(old_dosage, axis=0), ("row", "col")), 0)
     doubled = totals / (old_dosage.shape[0] * devices)
     spread = jnp.sqrt(doubled * (1.0 - 0.5 * doubled) + 0.1)
     usable = (jnp.arange(TILE)[None, :] < counts[:, None]).reshape(-1).astype(jnp.float32)

time: 157 us -> 155 us (0.987)
  waiting for transfers between devices: 67.9 us -> 64.3 us
  blocking collectives: 42 us -> 43.6 us
    all_gather x0 -> x1, blocking collectives: none -> 43.6 us  [on_device(): jax.lax.all_gather(jnp.sum(old_dosage, axis=0), ('row', 'col'))]
    psum x1 -> x0, blocking collectives: 42 us -> none  [on_device(): totals = lax.psum(jnp.sum(old_dosage, axis=0), ('row', 'col'))]
    all_gather x1, waiting for transfers between devices: 33.3 us -> 29.7 us  [on_device(): new_scores = lax.all_gather(scores_mine, 'row', axis=0, tiled=True)]
where the time goes in v1:
time: 155 us
  waiting for transfers between devices  64.3 us (41%)
  blocking collectives  43.6 us (28%)
  local copies, waits for them, and re-layouts  14.4 us (9%)
  matrix products  13.5 us (9%)
  between operations  13.4 us (9%)
  other arithmetic  5.77 us (4%)
    all_gather x1, blocking collectives, on_device(): jax.lax.all_gather(jnp.sum(old_dosage, axis=0), ('row', 'col'))  43.6 us
    all_gather x1, waiting for transfers between devices, on_device(): lax.all_gather(old_mine, 'col', axis=0, tiled=True)  34.6 us
    all_gather x1, waiting for transfers between devices, on_device(): new_scores = lax.all_gather(scores_mine, 'row', axis=0, tiled=True)  29.7 us
    dot_general x1, matrix products, on_device(): lax.dot_general(lax.all_gather(old_mine, 'col', axis=0, tiled=True), new_...  13.5 us
    unnamed x6, local copies, waits for them, and re-layouts  8.71 us
    mul x1, local copies, waits for them, and re-layouts, on_device(): masked_update = scaled * affected.astype(jnp.float32)[:, None, :, None]  5.45 us
  transfers between devices with their start and end apart: 2, of which 2 were waited for; matrix products, arithmetic and copies ran while one was open for 10% of the time, Pallas kernels for 0%

profile of v1, /device:TPU:0, one launch (start us, length us, event | category | flops | bytes accessed | tf_op | source)
XLA Modules:
  0.0 155.0 jit_solution(9454500989902597892)
XLA Ops:
  6.5 0.0 copy-start
  6.5 0.0 copy-start.1
  6.5 0.0 all-gather.6.cloned.1.call-start
  6.5 1.9 %reduce_sum.18 = f32[1024]{0:T(1024)S(1)} reduce(f32[512,1024]{1,0:T(8,128)} %param.6, f32[]{:T(128)} %constant.5.clone.1), dimensions={0}, to_apply=%region_0.0 | reduce | flops 523264 | bytes 2101252 | tf_op jit(solution)/shard_map/reduce_sum | solution.py:11
  8.4 43.6 %all-gather = f32[32768]{0:T(1024)S(1)} all-gather(f32[1024]{0:T(1024)S(1)} %reduce_sum.18), channel_id=2, replica_groups=mesh['row'=8,'col'=4] {'row','col'}, dimensions={0}, use_global_device_ids=true | all-gather | bytes 135168 | tf_op jit(solution)/shard_map/all_gather | solution.py:11
  52.1 0.7 fusion
  52.8 0.1 dynamic_slice.3
  52.9 1.8 %multiply_convert_fusion = bf16[128,1024]{1,0:T(8,128)(2,1)} fusion(f32[128,1024]{1,0:T(8,128)} %param.5, f32[128]{0:T(128)S(1)} %dynamic_slice.3, f32[1024]{0:T(1024)S(1)} %get-tuple-element.6, f32[1024]{0:T(1024)S(1)} %get-tuple-element.5), kind=kLoop, calls=%fused_computation.2 | loop fusion | flops 524288 | bytes 795136 | tf_op jit(solution)/shard_map/convert_element_type | solution.py:19
  54.8 0.0 all-gather.6.cloned.1.call-update
  54.8 0.0 all-gather.4.cloned.1.call-start
  54.8 0.0 copy-done
  54.8 1.3 divide_convert_fusion
  56.1 0.0 all-gather.4.cloned.1.call-update
  56.1 0.0 copy-done.1
  56.2 0.1 copy.8
  56.3 5.5 %mul.45 = f32[4,512,2,512]{3,2,1,0:T(2,128)} broadcast(f32[4,2]{1,0:T(4,128)S(1)} %copy.8), dimensions={0,2} | broadcast | bytes 8388640 | tf_op jit(solution)/shard_map/mul | solution.py:30
  61.7 8.7 %copy.10 = f32[256,8,2,512]{3,1,2,0:T(8,128)} copy(f32[256,8,2,512]{3,2,1,0:T(2,128)} %bitcast.8) | data formatting | bytes 16777216
  70.4 29.7 %all-gather.6.cloned.1.call-done = bf16[1024,1024]{1,0:T(8,128)(2,1)} async-done(((bf16[128,1024]{1,0:T(8,128)(2,1)}), bf16[1024,1024]{1,0:T(8,128)(2,1)}) %all-gather.6.cloned.1.call-update) | async-done | bytes 2097168 | tf_op jit(solution)/shard_map/all_gather | solution.py:20
  100.1 34.6 %all-gather.4.cloned.1.call-done = bf16[2048,1024]{1,0:T(8,128)(2,1)} async-done(((bf16[512,1024]{1,0:T(8,128)(2,1)}), bf16[2048,1024]{1,0:T(8,128)(2,1)}) %all-gather.4.cloned.1.call-update) | async-done | bytes 4194320 | tf_op jit(solution)/shard_map/all_gather | solution.py:23
  134.7 13.5 %add_convert_fusion = bf16[2048,1024]{1,0:T(8,128)(2,1)} fusion(f32[2048,1024]{1,0:T(8,128)} %bitcast.9, bf16[2048,1024]{1,0:T(8,128)(2,1)} %param.7, bf16[2048,1024]{1,0:T(8,128)(2,1)} %all-gather.4.cloned.1.call-done, bf16[1024,1024]{1,0:T(8,128)(2,1)} %all-gather.6.cloned.1.call-done), kind=kOutput, calls=%fused_computation | convolution fusion | flops 4305453056 | bytes 23068672 | tf_op jit(solution)/shard_map/dot_general | solution.py:22
  (5 shorter events, 0.1 us)
Async XLA Ops:
  6.5 48.3 %copy-start = (f32[512,1024]{1,0:T(8,128)S(1)}, f32[512,1024]{1,0:T(8,128)}, u32[]{:S(2)}) copy-start(f32[512,1024]{1,0:T(8,128)} %param.6) | copy-start | bytes 6291460
  6.5 49.6 %copy-start.1 = (s32[4,2]{0,1:T(2,128)S(1)}, s32[4,2]{0,1:T(2,128)}, u32[]{:S(2)}) copy-start(s32[4,2]{0,1:T(2,128)} %param.9) | copy-start | bytes 100
  6.5 93.6 %all-gather.6.cloned.1.call-start = ((), (), s32[]{:S(2)}) async-start(), calls=%async_computation.1 | async-start | bytes 2359296 | tf_op jit(solution)/shard_map/all_gather | solution.py:20
  54.8 79.9 %all-gather.4.cloned.1.call-start = ((), (), s32[]{:S(2)}) async-start(), calls=%async_computation | async-start | bytes 5242880 | tf_op jit(solution)/shard_map/all_gather | solution.py:23
Sparse Core Ops, SparseCore 0:
  54.9 45.1 all-gather.5
  101.7 32.9 all-gather.3
